TPU v7x, 32 devices: a whole 2x2x4 slice. The times are simulated.
32 devices in a mesh: gx: 4 (over y, core), gy: 8 (over z, x).
Axes of the slice: x: 2, y: 2, z: 4, core: 2. Of those that a mesh axis runs over, the one named last changes fastest.
Arguments:
- transfer: bfloat16 [512, 75, 128], P(('gx', 'gy')), may hold values from -6 to 6
- positions: float32 [512, 3, 128], P(('gx', 'gy')), may hold values from -4 to 4
- normals: float32 [512, 3, 128], P(('gx', 'gy')), may hold values from -4 to 4
- area: float32 [512, 128], P(('gx', 'gy')), may hold values from 0.06 to 3
- albedo: float32 [512, 3, 128], P(('gx', 'gy')), may hold values from 0.3 to 0.9
- pairs: int32 [512, 40], P(('gx', 'gy')), may hold values from 0 to 511, as said below
- home: int32 [512], replicated, may hold values from 0 to 511, as said below
Outputs:
- bounce_one: bfloat16 [512, 75, 128], P(('gx', 'gy'))
- bounce_two: bfloat16 [512, 75, 128], P(('gx', 'gy'))
- energies: float32 [2], replicated
Inputs may be any that keep to these rules, and one draw needn't show every extreme that they name: `home`: A permutation; the block in slot s is held by device s // 16, devices counted gx major. `pairs`: the first 16 entries of a row name blocks held by the same device as the row's slot, the other 24 name blocks held by other devices. Over the rows of one device, the far entries name at most 2 distinct blocks of any one other device, and exactly 2 of some. Ids may repeat within a row; each entry counts.
All inputs are finite; a program needn't handle non-finite values.
Results may differ from a plain program's by a relative error of at most 0.02.
Values may be sent and summed in bfloat16 or wider, within the bound.
A program may use at most 128 MiB of HBM per device.

v0:
```python
import jax
import jax.numpy as jnp
from jax import lax
from jax.sharding import PartitionSpec as P

COLORS = 3
NEAR = 16
CAP = 2


batch_blocks = 4


def form_tiles(recv_pos, recv_nrm, src_pos, src_nrm, src_area):
    distance = None
    along_p = None
    along_q = None
    for axis_id in range(3):
        gap_vec = src_pos[:, :, axis_id, None, :] - recv_pos[:, None, axis_id, :, None]
        near_term = recv_nrm[:, None, axis_id, :, None] * gap_vec
        far_term = src_nrm[:, :, axis_id, None, :] * gap_vec
        if distance is None:
            distance = gap_vec * gap_vec
            along_p = near_term
            along_q = far_term
        else:
            distance = distance + gap_vec * gap_vec
            along_p = along_p + near_term
            along_q = along_q + far_term
    soft_sq = distance + 1.0
    transfer_factors = (
        jnp.maximum(along_p, 0.0)
        * jnp.maximum(-along_q, 0.0)
        * src_area[:, :, None, :]
        / (jnp.pi * soft_sq * soft_sq)
    )
    return transfer_factors.astype(jnp.bfloat16)


def build_tiles(src_positions, src_normals, src_area, pair_row_list, recv_positions, recv_normals):
    turns = pair_row_list.shape[0] // batch_blocks

    def group_tiles(group_id):
        first_row = group_id * batch_blocks
        picked_rows = lax.dynamic_slice_in_dim(pair_row_list, first_row, batch_blocks, 0)
        recv_pos = lax.dynamic_slice_in_dim(recv_positions, first_row, batch_blocks, 0)
        recv_nrm = lax.dynamic_slice_in_dim(recv_normals, first_row, batch_blocks, 0)
        return form_tiles(
            recv_pos,
            recv_nrm,
            jnp.take(src_positions, picked_rows, axis=0),
            jnp.take(src_normals, picked_rows, axis=0),
            jnp.take(src_area, picked_rows, axis=0),
        )

    return lax.map(group_tiles, jnp.arange(turns, dtype=jnp.int32))


def apply_tiles(source_rows, pair_row_list, tiles):
    turns = tiles.shape[0]
    grouped_rows = pair_row_list.reshape((turns, batch_blocks) + pair_row_list.shape[1:])

    def group_term(operands):
        picked_rows, transfer_factors = operands
        collected_values = jnp.take(source_rows, picked_rows, axis=0)
        return jnp.einsum(
            "wxmy,wxsy->wms", collected_values, transfer_factors, preferred_element_type=jnp.float32
        )

    summed = lax.map(group_term, (grouped_rows, tiles))
    return summed.reshape((pair_row_list.shape[0],) + source_rows.shape[1:])


def apply_albedo(summed, albedo):
    blocks_here, channels, verts = summed.shape
    shaped = summed.reshape(blocks_here, COLORS, channels // COLORS, verts) * albedo[:, :, None, :]
    return shaped.reshape(blocks_here, channels, verts)


def total_energy(local_part):
    return lax.psum(local_part, ("gx", "gy"))


def body(transfer, positions, normals, area, albedo, pairs, home):
    devices_all = lax.axis_size(("gx", "gy"))
    device_id = lax.axis_index(("gx", "gy"))
    per_device = transfer.shape[0]
    slot_ids = jnp.take(home, pairs, axis=0)
    near_rows = slot_ids[:, :NEAR] - device_id * per_device
    distant_slot_ids = slot_ids[:, NEAR:]
    owner_dev = distant_slot_ids // per_device
    flat_need = (
        jnp.zeros((devices_all * per_device,), jnp.int32).at[distant_slot_ids.reshape(-1)].max(1)
    )
    needed = flat_need.reshape(devices_all, per_device)
    rank_in_owner = jnp.cumsum(needed, axis=1) - 1
    picked = (
        (needed[:, :, None] == 1)
        & (rank_in_owner[:, :, None] == jnp.arange(CAP, dtype=jnp.int32)[None, None, :])
    ).astype(jnp.int32)
    filled = jnp.sum(picked, axis=1)
    request_list = jnp.sum(
        picked * jnp.arange(per_device, dtype=jnp.int32)[None, :, None], axis=1
    ) + per_device * (1 - filled)
    far_rows = owner_dev * CAP + jnp.take(rank_in_owner.reshape(-1), distant_slot_ids)
    incident_radiance = lax.all_to_all(
        request_list, ("gx", "gy"), split_axis=0, concat_axis=0, tiled=True
    )
    is_filled = incident_radiance < per_device
    chosen = jnp.minimum(incident_radiance, per_device - 1)

    def outbound(table):
        collected_values = jnp.take(table, chosen, axis=0)
        retain_mask = is_filled.reshape(is_filled.shape + (1,) * (table.ndim - 1))
        return jnp.where(retain_mask, collected_values, jnp.zeros((), table.dtype))

    def direct_table(table):
        return table.reshape((devices_all * CAP,) + table.shape[2:])

    near_tiles = build_tiles(positions, normals, area, near_rows, positions, normals)
    near_first = apply_tiles(transfer, near_rows, near_tiles)
    exitant_radiance = (outbound(transfer), outbound(positions), outbound(normals), outbound(area))
    arrived = (
        lax.all_to_all(exitant_radiance[0], ("gx", "gy"), split_axis=0, concat_axis=0, tiled=True),
        lax.all_to_all(
            exitant_radiance[1].astype(jnp.bfloat16),
            ("gx", "gy"),
            split_axis=0,
            concat_axis=0,
            tiled=True,
        ).astype(jnp.float32),
        lax.all_to_all(
            exitant_radiance[2].astype(jnp.bfloat16),
            ("gx", "gy"),
            split_axis=0,
            concat_axis=0,
            tiled=True,
        ).astype(jnp.float32),
        lax.all_to_all(
            exitant_radiance[3].astype(jnp.bfloat16),
            ("gx", "gy"),
            split_axis=0,
            concat_axis=0,
            tiled=True,
        ).astype(jnp.float32),
    )
    table_transfer = direct_table(arrived[0])
    table_pos = direct_table(arrived[1])
    table_nrm = direct_table(arrived[2])
    table_area = direct_table(arrived[3])
    far_tiles = build_tiles(table_pos, table_nrm, table_area, far_rows, positions, normals)
    far_first = apply_tiles(table_transfer, far_rows, far_tiles)
    first_bounce = apply_albedo(near_first + far_first, albedo)
    bounce_one = first_bounce.astype(jnp.bfloat16)
    local_one = jnp.sum(area[:, None, :] * first_bounce * first_bounce)
    near_second = apply_tiles(bounce_one, near_rows, near_tiles)
    second_table = direct_table(
        lax.all_to_all(outbound(bounce_one), ("gx", "gy"), split_axis=0, concat_axis=0, tiled=True)
    )
    far_second = apply_tiles(second_table, far_rows, far_tiles)
    second_bounce = apply_albedo(near_second + far_second, albedo)
    bounce_two = second_bounce.astype(jnp.bfloat16)
    local_two = jnp.sum(area[:, None, :] * second_bounce * second_bounce)
    energy_one = total_energy(local_one)
    energy_two = total_energy(local_two)
    inv_count = 1.0 / (devices_all * per_device * transfer.shape[2] * transfer.shape[1])
    energies = jnp.stack([energy_one, energy_two]) * inv_count
    return (bounce_one, bounce_two, energies)


def solution(mesh):
    return jax.shard_map(
        body,
        mesh=mesh,
        in_specs=(
            P(("gx", "gy"), None, None),
            P(("gx", "gy"), None, None),
            P(("gx", "gy"), None, None),
            P(("gx", "gy"), None),
            P(("gx", "gy"), None, None),
            P(("gx", "gy"), None),
            P(),
        ),
        out_specs=(P(("gx", "gy"), None, None), P(("gx", "gy"), None, None), P()),
        check_vma=False,
    )
```

profile of v0, /device:TPU:0, one launch (start us, length us, event | category | flops | bytes accessed | tf_op | source)
XLA Modules:
  0.0 292.2 jit_solution(17152638488114444716)
XLA Ops:
  1.5 4.3 %gather_fusion.10 = s32[640]{0:T(1024)S(1)} fusion(s32[512]{0:T(512)S(1)} %copy-done, s32[1024]{0:T(1024)S(1)} %pad_clamp_fusion.9), kind=kCustom, calls=%fused_computation.14 | custom fusion | bytes 7680 | tf_op jit(solution)/shard_map/jit(_take)/gather | solution.py:88
  6.1 3.9 %scatter_custom_fusion = s32[512]{0:T(512)S(1)} fusion(s32[384]{0:T(512)S(1)} %fusion.94, s32[384]{0:T(512)S(1)} %broadcast.438, s32[]{:T(128)} %copy.344), kind=kCustom, calls=%fused_computation.200 | custom fusion | flops 384 | bytes 2052 | tf_op jit(solution)/shard_map/scatter-max | solution.py:93
  11.2 7.3 %all-to-all-start = ((s32[32,1,2]{2,1,0:T(1,128)}), s32[32,1,2]{2,1,0:T(1,128)S(1)}, u32[]{:S(2)}, u32[]{:S(2)}) async-start(s32[32,1,2]{2,1,0:T(1,128)} %copy.220), calls=%async_computation | async-start | bytes 32768 | tf_op jit(solution)/shard_map/all_to_all | solution.py:106
  18.7 2.8 gather_fusion.11
  21.7 38.1 %while.60 = (s32[]{:T(128)}, bf16[4,4,16,128,128]{4,3,2,1,0:T(8,128)(2,1)}, s32[4]{0:T(128)S(1)}, f32[16,3,128]{2,1,0:T(4,128)S(1)}, s32[16,16]{1,0:T(8,128)S(1)...) while((s32[]{:T(128)}, ...), condition=%wide.region_1.3_spmd, body=%wide.region_0.0_spmd.sunk | while | flops 29418888 | bytes 3681183 | solution.py:56
  25.4 5.8 %fusion.115 = bf16[4,4,16,128,128]{4,3,2,1,0:T(8,128)(2,1)} fusion(bf16[4,4,16,128,128]{4,3,2,1,0:T(8,128)(2,1)} %get-tuple-element.810, s32[]{:T(128)} %get-tuple-element.809, f32[4,16,128]{2,1,0:T(8,128)S(1)} %broadcast_select_fusion.11, f32[4,16,128]{2,1,0:T(8,128)S(1)} %bitcast.220, f32[4,16,128]{2,1,0:T(8,128)S(1)} %bitcast.219, ...), kind=kLoop, calls=%fused_computation.42.clone.1 | loop fusion | flops 29360128 | bytes 2339328 | tf_op jit(solution)/shard_map/while/body/jit(dynamic_update_index_in_dim)/dynamic_update_slice | solution.py:56
  35.0 5.8 %fusion.115 = bf16[4,4,16,128,128]{4,3,2,1,0:T(8,128)(2,1)} fusion(bf16[4,4,16,128,128]{4,3,2,1,0:T(8,128)(2,1)} %get-tuple-element.810, s32[]{:T(128)} %get-tuple-element.809, f32[4,16,128]{2,1,0:T(8,128)S(1)} %broadcast_select_fusion.11, f32[4,16,128]{2,1,0:T(8,128)S(1)} %bitcast.220, f32[4,16,128]{2,1,0:T(8,128)S(1)} %bitcast.219, ...), kind=kLoop, calls=%fused_computation.42.clone.1 | loop fusion | flops 29360128 | bytes 2339328 | tf_op jit(solution)/shard_map/while/body/jit(dynamic_update_index_in_dim)/dynamic_update_slice | solution.py:56
  44.5 5.8 %fusion.115 = bf16[4,4,16,128,128]{4,3,2,1,0:T(8,128)(2,1)} fusion(bf16[4,4,16,128,128]{4,3,2,1,0:T(8,128)(2,1)} %get-tuple-element.810, s32[]{:T(128)} %get-tuple-element.809, f32[4,16,128]{2,1,0:T(8,128)S(1)} %broadcast_select_fusion.11, f32[4,16,128]{2,1,0:T(8,128)S(1)} %bitcast.220, f32[4,16,128]{2,1,0:T(8,128)S(1)} %bitcast.219, ...), kind=kLoop, calls=%fused_computation.42.clone.1 | loop fusion | flops 29360128 | bytes 2339328 | tf_op jit(solution)/shard_map/while/body/jit(dynamic_update_index_in_dim)/dynamic_update_slice | solution.py:56
  54.0 5.8 %fusion.115 = bf16[4,4,16,128,128]{4,3,2,1,0:T(8,128)(2,1)} fusion(bf16[4,4,16,128,128]{4,3,2,1,0:T(8,128)(2,1)} %get-tuple-element.810, s32[]{:T(128)} %get-tuple-element.809, f32[4,16,128]{2,1,0:T(8,128)S(1)} %broadcast_select_fusion.11, f32[4,16,128]{2,1,0:T(8,128)S(1)} %bitcast.220, f32[4,16,128]{2,1,0:T(8,128)S(1)} %bitcast.219, ...), kind=kLoop, calls=%fused_computation.42.clone.1 | loop fusion | flops 29360128 | bytes 2339328 | tf_op jit(solution)/shard_map/while/body/jit(dynamic_update_index_in_dim)/dynamic_update_slice | solution.py:56
  60.0 14.0 %while.61 = (s32[]{:T(128)}, f32[4,4,75,128]{3,1,0,2:T(4,128)S(1)}, s32[4,4,16]{2,1,0:T(4,128)S(1)}, bf16[16,75,128]{2,1,0:T(8,128)(2,1)S(1)}, bf16[4,4,16,128,128]{4,3,2,1,0:T(8,128)(2,1)}, /*index=5*/s32[]{:T(128)}) while((s32[]{:T(128)}, f32[4,4,75,128]{3,1,0,2:T(4,128)S(1)}, s32[4,4,16]{2,1,0:T(4,128)S(1)}, ...), condition=%wide.region_3.6_spmd, body=%wide.region_2.5_spmd.sunk | while | flops 157902208 | bytes 6260941 | solution.py:70
  60.9 2.5 fusion.118
  64.4 2.5 fusion.118
  67.9 2.5 fusion.118
  71.4 2.5 fusion.118
  77.6 6.0 %all-to-all-start.4 = ((bf16[32,2,128]{2,1,0:T(2,128)(2,1)}), bf16[32,2,128]{2,1,0:T(2,128)(2,1)S(1)}, u32[]{:S(2)}, u32[]{:S(2)}) async-start(bf16[32,2,128]{2,1,0:T(2,128)(2,1)} %select_convert_fusion), calls=%async_computation.4 | async-start | bytes 32768 | tf_op jit(solution)/shard_map/all_to_all | solution.py:139
  84.5 5.4 %gather_fusion.13 = bf16[64,75,128]{2,0,1:T(8,128)(2,1)S(1)} fusion(bf16[16,75,128]{2,0,1:T(8,128)(2,1)S(1)} %copy-done.1, s32[1024]{0:T(1024)S(1)} %pad_clamp_fusion.7), kind=kCustom, calls=%fused_computation.4.clone | custom fusion | bytes 2457856 | tf_op jit(solution)/shard_map/jit(_take)/gather | solution.py:113
  90.6 5.0 %all-to-all-start.2 = ((bf16[32,2,3,128]{3,1,2,0:T(2,128)(2,1)}), bf16[32,2,3,128]{3,1,2,0:T(2,128)(2,1)S(1)}, u32[]{:S(2)}, u32[]{:S(2)}) async-start(bf16[32,2,3,128]{3,1,2,0:T(2,128)(2,1)} %get-tuple-element.491), calls=%async_computation.2 | async-start | bytes 98304 | tf_op jit(solution)/shard_map/all_to_all | solution.py:125
  95.6 2.5 broadcast_select_fusion.7
  98.1 4.7 %all-to-all-done.2 = bf16[32,2,3,128]{3,1,2,0:T(2,128)(2,1)S(1)} async-done(((bf16[32,2,3,128]{3,1,2,0:T(2,128)(2,1)}), bf16[32,2,3,128]{3,1,2,0:T(2,128)(2,1)S(1)}, u32[]{:S(2)}, u32[]{:S(2)}) %all-to-all-start.2) | async-done | bytes 49184 | tf_op jit(solution)/shard_map/all_to_all | solution.py:125
  102.9 2.6 all-to-all-start.3
  105.6 7.1 %all-to-all-done.3 = bf16[32,2,3,128]{3,1,2,0:T(2,128)(2,1)S(1)} async-done(((bf16[32,2,3,128]{3,1,2,0:T(2,128)(2,1)}), bf16[32,2,3,128]{3,1,2,0:T(2,128)(2,1)S(1)}, u32[]{:S(2)}, u32[]{:S(2)}) %all-to-all-start.3) | async-done | bytes 49184 | tf_op jit(solution)/shard_map/all_to_all | solution.py:132
  112.7 2.9 all-to-all-start.1
  115.8 43.3 %while.62 = (s32[]{:T(128)}, bf16[4,4,24,128,128]{4,3,2,1,0:T(8,128)(2,1)}, s32[4]{0:T(128)S(1)}, f32[16,3,128]{2,0,1:T(8,128)S(1)}, s32[16,24]{1,0:T(8,128)S(1)...) while((s32[]{:T(128)}, ...), condition=%wide.region_9.14_spmd, body=%wide.region_8.13_spmd.sunk | while | flops 44127816 | bytes 5500943 | solution.py:56
  119.4 7.2 %fusion.119 = bf16[4,4,24,128,128]{4,3,2,1,0:T(8,128)(2,1)} fusion(bf16[4,4,24,128,128]{4,3,2,1,0:T(8,128)(2,1)} %get-tuple-element.869, s32[]{:T(128)} %get-tuple-element.868, f32[4,24,128]{2,1,0:T(8,128)S(1)} %broadcast_select_fusion.13, f32[4,24,128]{2,1,0:T(8,128)S(1)} %get-tuple-element.763, f32[4,24,128]{2,1,0:T(8,128)S(1)} %get-tuple-element.764, ...), kind=kLoop, calls=%fused_computation.92.clone.1 | loop fusion | flops 44040192 | bytes 3502592 | tf_op jit(solution)/shard_map/while/body/jit(dynamic_update_index_in_dim)/dynamic_update_slice | solution.py:56
  130.2 7.2 %fusion.119 = bf16[4,4,24,128,128]{4,3,2,1,0:T(8,128)(2,1)} fusion(bf16[4,4,24,128,128]{4,3,2,1,0:T(8,128)(2,1)} %get-tuple-element.869, s32[]{:T(128)} %get-tuple-element.868, f32[4,24,128]{2,1,0:T(8,128)S(1)} %broadcast_select_fusion.13, f32[4,24,128]{2,1,0:T(8,128)S(1)} %get-tuple-element.763, f32[4,24,128]{2,1,0:T(8,128)S(1)} %get-tuple-element.764, ...), kind=kLoop, calls=%fused_computation.92.clone.1 | loop fusion | flops 44040192 | bytes 3502592 | tf_op jit(solution)/shard_map/while/body/jit(dynamic_update_index_in_dim)/dynamic_update_slice | solution.py:56
  141.0 7.2 %fusion.119 = bf16[4,4,24,128,128]{4,3,2,1,0:T(8,128)(2,1)} fusion(bf16[4,4,24,128,128]{4,3,2,1,0:T(8,128)(2,1)} %get-tuple-element.869, s32[]{:T(128)} %get-tuple-element.868, f32[4,24,128]{2,1,0:T(8,128)S(1)} %broadcast_select_fusion.13, f32[4,24,128]{2,1,0:T(8,128)S(1)} %get-tuple-element.763, f32[4,24,128]{2,1,0:T(8,128)S(1)} %get-tuple-element.764, ...), kind=kLoop, calls=%fused_computation.92.clone.1 | loop fusion | flops 44040192 | bytes 3502592 | tf_op jit(solution)/shard_map/while/body/jit(dynamic_update_index_in_dim)/dynamic_update_slice | solution.py:56
  151.9 7.2 %fusion.119 = bf16[4,4,24,128,128]{4,3,2,1,0:T(8,128)(2,1)} fusion(bf16[4,4,24,128,128]{4,3,2,1,0:T(8,128)(2,1)} %get-tuple-element.869, s32[]{:T(128)} %get-tuple-element.868, f32[4,24,128]{2,1,0:T(8,128)S(1)} %broadcast_select_fusion.13, f32[4,24,128]{2,1,0:T(8,128)S(1)} %get-tuple-element.763, f32[4,24,128]{2,1,0:T(8,128)S(1)} %get-tuple-element.764, ...), kind=kLoop, calls=%fused_computation.92.clone.1 | loop fusion | flops 44040192 | bytes 3502592 | tf_op jit(solution)/shard_map/while/body/jit(dynamic_update_index_in_dim)/dynamic_update_slice | solution.py:56
  162.2 19.6 %while.63 = (s32[]{:T(128)}, f32[4,4,75,128]{3,1,0,2:T(4,128)}, s32[4,4,24]{2,1,0:T(4,128)S(1)}, bf16[64,75,128]{2,1,0:T(8,128)(2,1)S(1)}, bf16[4,4,24,128,128]{4,3,2,1,0:T(8,128)(2,1)}, /*index=5*/s32[]{:T(128)}) while((s32[]{:T(128)}, f32[4,4,75,128]{3,1,0,2:T(4,128)}, s32[4,4,24]{2,1,0:T(4,128)S(1)}, ...), condition=%wide.region_11.18_spmd, body=%wide.region_10.17_spmd.sunk | while | flops 236852800 | bytes 9143817 | solution.py:70
  163.2 3.1 %fusion.122 = f32[1,4,75,128]{3,2,1,0:T(8,128)S(1)} fusion(bf16[4,4,24,128,128]{4,3,2,1,0:T(8,128)(2,1)} %get-tuple-element.914, s32[]{:T(128)} %get-tuple-element.904, bf16[4,24,75,128]{3,2,1,0:T(8,128)(2,1)S(1)} %bitcast.201, pred[4,24]{1,0:T(4,128)(4,1)S(1)} %get-tuple-element.781), kind=kOutput, calls=%fused_computation.116.clone.1 | convolution fusion | flops 236851200 | bytes 5143136 | tf_op jit(solution)/shard_map/while/body/eval_jaxpr/wxmy,wxsy->wms/dot_general | solution.py:66
  168.1 3.1 %fusion.122 = f32[1,4,75,128]{3,2,1,0:T(8,128)S(1)} fusion(bf16[4,4,24,128,128]{4,3,2,1,0:T(8,128)(2,1)} %get-tuple-element.914, s32[]{:T(128)} %get-tuple-element.904, bf16[4,24,75,128]{3,2,1,0:T(8,128)(2,1)S(1)} %bitcast.201, pred[4,24]{1,0:T(4,128)(4,1)S(1)} %get-tuple-element.781), kind=kOutput, calls=%fused_computation.116.clone.1 | convolution fusion | flops 236851200 | bytes 5143136 | tf_op jit(solution)/shard_map/while/body/eval_jaxpr/wxmy,wxsy->wms/dot_general | solution.py:66
  173.0 3.1 %fusion.122 = f32[1,4,75,128]{3,2,1,0:T(8,128)S(1)} fusion(bf16[4,4,24,128,128]{4,3,2,1,0:T(8,128)(2,1)} %get-tuple-element.914, s32[]{:T(128)} %get-tuple-element.904, bf16[4,24,75,128]{3,2,1,0:T(8,128)(2,1)S(1)} %bitcast.201, pred[4,24]{1,0:T(4,128)(4,1)S(1)} %get-tuple-element.781), kind=kOutput, calls=%fused_computation.116.clone.1 | convolution fusion | flops 236851200 | bytes 5143136 | tf_op jit(solution)/shard_map/while/body/eval_jaxpr/wxmy,wxsy->wms/dot_general | solution.py:66
  177.9 3.1 %fusion.122 = f32[1,4,75,128]{3,2,1,0:T(8,128)S(1)} fusion(bf16[4,4,24,128,128]{4,3,2,1,0:T(8,128)(2,1)} %get-tuple-element.914, s32[]{:T(128)} %get-tuple-element.904, bf16[4,24,75,128]{3,2,1,0:T(8,128)(2,1)S(1)} %bitcast.201, pred[4,24]{1,0:T(4,128)(4,1)S(1)} %get-tuple-element.781), kind=kOutput, calls=%fused_computation.116.clone.1 | convolution fusion | flops 236851200 | bytes 5143136 | tf_op jit(solution)/shard_map/while/body/eval_jaxpr/wxmy,wxsy->wms/dot_general | solution.py:66
  186.7 2.6 broadcast_select_fusion.6
  189.3 5.9 %all-to-all-start.5 = ((bf16[32,2,75,128]{3,1,2,0:T(2,128)(2,1)}), bf16[32,2,75,128]{3,1,2,0:T(2,128)(2,1)S(1)}, u32[]{:S(2)}, u32[]{:S(2)}) async-start(bf16[32,2,75,128]{3,1,2,0:T(2,128)(2,1)} %broadcast_select_fusion.6), calls=%async_computation.5 | async-start | bytes 2457600 | tf_op jit(solution)/shard_map/all_to_all | solution.py:158
  195.3 14.0 %while.64 = (s32[]{:T(128)}, f32[4,4,75,128]{3,1,0,2:T(4,128)S(1)}, s32[4,4,16]{2,1,0:T(4,128)S(1)}, bf16[16,75,128]{2,1,0:T(8,128)(2,1)S(1)}, bf16[4,4,16,128,128]{4,3,2,1,0:T(8,128)(2,1)}, /*index=5*/s32[]{:T(128)}) while((s32[]{:T(128)}, f32[4,4,75,128]{3,1,0,2:T(4,128)S(1)}, s32[4,4,16]{2,1,0:T(4,128)S(1)}, ...), condition=%wide.region_13.20_spmd, body=%wide.region_12.19_spmd.sunk | while | flops 157902208 | bytes 6260941 | solution.py:70
  196.2 2.5 fusion.125
  199.7 2.5 fusion.125
  203.2 2.5 fusion.125
  206.7 2.5 fusion.125
  209.3 16.9 %all-to-all-done.5 = bf16[32,2,75,128]{3,1,2,0:T(2,128)(2,1)S(1)} async-done(((bf16[32,2,75,128]{3,1,2,0:T(2,128)(2,1)}), bf16[32,2,75,128]{3,1,2,0:T(2,128)(2,1)S(1)}, u32[]{:S(2)}, u32[]{:S(2)}) %all-to-all-start.5) | async-done | bytes 1228832 | tf_op jit(solution)/shard_map/all_to_all | solution.py:158
  229.3 19.6 %while.65 = (s32[]{:T(128)}, f32[4,4,75,128]{3,1,0,2:T(4,128)}, s32[4,4,24]{2,1,0:T(4,128)S(1)}, bf16[64,75,128]{2,1,0:T(8,128)(2,1)S(1)}, bf16[4,4,24,128,128]{4,3,2,1,0:T(8,128)(2,1)}, /*index=5*/s32[]{:T(128)}) while((s32[]{:T(128)}, f32[4,4,75,128]{3,1,0,2:T(4,128)}, s32[4,4,24]{2,1,0:T(4,128)S(1)}, ...), condition=%wide.region_15.22_spmd, body=%wide.region_14.21_spmd.sunk | while | flops 236852800 | bytes 9143817 | solution.py:70
  230.4 3.1 %fusion.128 = f32[1,4,75,128]{3,2,1,0:T(8,128)S(1)} fusion(bf16[4,4,24,128,128]{4,3,2,1,0:T(8,128)(2,1)} %get-tuple-element.950, s32[]{:T(128)} %get-tuple-element.940, bf16[4,24,75,128]{3,2,1,0:T(8,128)(2,1)S(1)} %bitcast.202, pred[4,24]{1,0:T(4,128)(4,1)S(1)} %get-tuple-element.795), kind=kOutput, calls=%fused_computation.142.clone.1 | convolution fusion | flops 236851200 | bytes 5143136 | tf_op jit(solution)/shard_map/while/body/eval_jaxpr/wxmy,wxsy->wms/dot_general | solution.py:66
  235.3 3.1 %fusion.128 = f32[1,4,75,128]{3,2,1,0:T(8,128)S(1)} fusion(bf16[4,4,24,128,128]{4,3,2,1,0:T(8,128)(2,1)} %get-tuple-element.950, s32[]{:T(128)} %get-tuple-element.940, bf16[4,24,75,128]{3,2,1,0:T(8,128)(2,1)S(1)} %bitcast.202, pred[4,24]{1,0:T(4,128)(4,1)S(1)} %get-tuple-element.795), kind=kOutput, calls=%fused_computation.142.clone.1 | convolution fusion | flops 236851200 | bytes 5143136 | tf_op jit(solution)/shard_map/while/body/eval_jaxpr/wxmy,wxsy->wms/dot_general | solution.py:66
  240.2 3.1 %fusion.128 = f32[1,4,75,128]{3,2,1,0:T(8,128)S(1)} fusion(bf16[4,4,24,128,128]{4,3,2,1,0:T(8,128)(2,1)} %get-tuple-element.950, s32[]{:T(128)} %get-tuple-element.940, bf16[4,24,75,128]{3,2,1,0:T(8,128)(2,1)S(1)} %bitcast.202, pred[4,24]{1,0:T(4,128)(4,1)S(1)} %get-tuple-element.795), kind=kOutput, calls=%fused_computation.142.clone.1 | convolution fusion | flops 236851200 | bytes 5143136 | tf_op jit(solution)/shard_map/while/body/eval_jaxpr/wxmy,wxsy->wms/dot_general | solution.py:66
  245.1 3.1 %fusion.128 = f32[1,4,75,128]{3,2,1,0:T(8,128)S(1)} fusion(bf16[4,4,24,128,128]{4,3,2,1,0:T(8,128)(2,1)} %get-tuple-element.950, s32[]{:T(128)} %get-tuple-element.940, bf16[4,24,75,128]{3,2,1,0:T(8,128)(2,1)S(1)} %bitcast.202, pred[4,24]{1,0:T(4,128)(4,1)S(1)} %get-tuple-element.795), kind=kOutput, calls=%fused_computation.142.clone.1 | convolution fusion | flops 236851200 | bytes 5143136 | tf_op jit(solution)/shard_map/while/body/eval_jaxpr/wxmy,wxsy->wms/dot_general | solution.py:66
  248.9 2.7 fusion.83
  252.4 37.9 %all-reduce = (f32[1]{0:T(128)}, f32[1]{0:T(128)}) all-reduce(f32[1]{0:T(128)} %bitcast.78, f32[1]{0:T(128)} %bitcast.77), channel_id=1, replica_groups=mesh['gx'=4,'gy'=8] {'gx','gy'}, use_global_device_ids=true, to_apply=%region_19.26 | all-reduce | flops 2 | bytes 16 | tf_op jit(solution)/shard_map/psum | solution.py:81
  290.4 1.8 maximum_multiply_fusion
  (264 shorter events, 65.9 us)
Async XLA Ops:
  0.6 0.8 copy-start
  1.5 4.4 %copy-start.10 = (s32[16,40]{1,0:T(8,128)S(1)}, s32[16,40]{1,0:T(8,128)}, u32[]{:S(2)}) copy-start(s32[16,40]{1,0:T(8,128)} %param.36) | copy-start | bytes 7684
  11.2 63.0 %all-to-all-start = ((s32[32,1,2]{2,1,0:T(1,128)}), s32[32,1,2]{2,1,0:T(1,128)S(1)}, u32[]{:S(2)}, u32[]{:S(2)}) async-start(s32[32,1,2]{2,1,0:T(1,128)} %copy.220), calls=%async_computation | async-start | bytes 32768 | tf_op jit(solution)/shard_map/all_to_all | solution.py:106
  18.7 3.0 %copy-start.3 = (f32[16,3,128]{2,0,1:T(8,128)S(1)}, f32[16,3,128]{2,0,1:T(8,128)}, u32[]{:S(2)}) copy-start(f32[16,3,128]{2,0,1:T(8,128)} %param.33) | copy-start | bytes 73732
  18.7 3.0 %copy-start.4 = (f32[16,3,128]{2,0,1:T(8,128)S(1)}, f32[16,3,128]{2,0,1:T(8,128)}, u32[]{:S(2)}) copy-start(f32[16,3,128]{2,0,1:T(8,128)} %param.32) | copy-start | bytes 73732
  18.7 3.0 %copy-start.2 = (f32[16,128]{1,0:T(8,128)S(1)}, f32[16,128]{1,0:T(8,128)}, u32[]{:S(2)}) copy-start(f32[16,128]{1,0:T(8,128)} %param.34) | copy-start | bytes 24580
  21.7 38.1 %copy-start.1 = (bf16[16,75,128]{2,0,1:T(8,128)(2,1)S(1)}, bf16[16,75,128]{2,0,1:T(8,128)(2,1)}, u32[]{:S(2)}) copy-start(bf16[16,75,128]{2,0,1:T(8,128)(2,1)} %param.31) | copy-start | bytes 921604
  74.0 15.9 %copy-start.7 = (f32[4,4,75,128]{3,1,0,2:T(4,128)}, f32[4,4,75,128]{3,1,0,2:T(4,128)S(1)}, u32[]{:S(2)}) copy-start(f32[4,4,75,128]{3,1,0,2:T(4,128)S(1)} %get-tuple-element.202) | copy-start | bytes 1843204
  77.6 13.0 %all-to-all-start.4 = ((bf16[32,2,128]{2,1,0:T(2,128)(2,1)}), bf16[32,2,128]{2,1,0:T(2,128)(2,1)S(1)}, u32[]{:S(2)}, u32[]{:S(2)}) async-start(bf16[32,2,128]{2,1,0:T(2,128)(2,1)} %select_convert_fusion), calls=%async_computation.4 | async-start | bytes 32768 | tf_op jit(solution)/shard_map/all_to_all | solution.py:139
  90.6 12.2 %all-to-all-start.2 = ((bf16[32,2,3,128]{3,1,2,0:T(2,128)(2,1)}), bf16[32,2,3,128]{3,1,2,0:T(2,128)(2,1)S(1)}, u32[]{:S(2)}, u32[]{:S(2)}) async-start(bf16[32,2,3,128]{3,1,2,0:T(2,128)(2,1)} %get-tuple-element.491), calls=%async_computation.2 | async-start | bytes 98304 | tf_op jit(solution)/shard_map/all_to_all | solution.py:125
  102.9 9.8 %all-to-all-start.3 = ((bf16[32,2,3,128]{3,1,2,0:T(2,128)(2,1)}), bf16[32,2,3,128]{3,1,2,0:T(2,128)(2,1)S(1)}, u32[]{:S(2)}, u32[]{:S(2)}) async-start(bf16[32,2,3,128]{3,1,2,0:T(2,128)(2,1)} %get-tuple-element.490), calls=%async_computation.3 | async-start | bytes 98304 | tf_op jit(solution)/shard_map/all_to_all | solution.py:132
  112.7 46.4 %all-to-all-start.1 = ((bf16[32,2,75,128]{3,1,2,0:T(2,128)(2,1)}), bf16[32,2,75,128]{3,1,2,0:T(2,128)(2,1)S(1)}, u32[]{:S(2)}, u32[]{:S(2)}) async-start(bf16[32,2,75,128]{3,1,2,0:T(2,128)(2,1)} %broadcast_select_fusion.7), calls=%async_computation.1 | async-start | bytes 2457600 | tf_op jit(solution)/shard_map/all_to_all | solution.py:124
  162.2 21.3 %copy-start.9 = (f32[16,3,128]{2,0,1:T(8,128)S(1)}, f32[16,3,128]{2,0,1:T(8,128)}, u32[]{:S(2)}) copy-start(f32[16,3,128]{2,0,1:T(8,128)} %param.35) | copy-start | bytes 73732
  183.2 0.8 copy-start.5
  184.1 0.8 copy-start.6
  189.3 37.0 %all-to-all-start.5 = ((bf16[32,2,75,128]{3,1,2,0:T(2,128)(2,1)}), bf16[32,2,75,128]{3,1,2,0:T(2,128)(2,1)S(1)}, u32[]{:S(2)}, u32[]{:S(2)}) async-start(bf16[32,2,75,128]{3,1,2,0:T(2,128)(2,1)} %broadcast_select_fusion.6), calls=%async_computation.5 | async-start | bytes 2457600 | tf_op jit(solution)/shard_map/all_to_all | solution.py:158
  209.3 20.0 %copy-start.8 = (f32[4,4,75,128]{3,1,0,2:T(4,128)}, f32[4,4,75,128]{3,1,0,2:T(4,128)S(1)}, u32[]{:S(2)}) copy-start(f32[4,4,75,128]{3,1,0,2:T(4,128)S(1)} %get-tuple-element.205) | copy-start | bytes 1843204
where the time goes:
time: 293 us; the launch traced here: 292 us
  other arithmetic  72.8 us (25%)
  local copies, waits for them, and re-layouts  70.5 us (24%)
  matrix products  44.8 us (15%)
  blocking collectives  37.9 us (13%)
  starting transfers between devices  29.7 us (10%)
  waiting for transfers between devices  29.4 us (10%)
  loops' own time  5.89 us (2%)
    dynamic_update_slice x8, other arithmetic, build_tiles(): return lax.map(group_tiles, jnp.arange(turns, dtype=jnp.int32))  52.1 us
    dot_general x16, matrix products, group_term(): jnp.einsum('wxmy,wxsy->wms', collected_values, transfer_factors, preferre...  44.8 us
    psum x1, blocking collectives, total_energy(): return lax.psum(local_part, ('gx', 'gy'))  37.9 us
    all_to_all x1, waiting for transfers between devices, body(): lax.all_to_all(outbound(bounce_one), ('gx', 'gy'), split_axis=0, concat_a...  16.9 us
    gather x16, local copies, waits for them, and re-layouts, group_term(): collected_values = jnp.take(source_rows, picked_rows, axis=0)  13.9 us
    gather x5, local copies, waits for them, and re-layouts, outbound(): collected_values = jnp.take(table, chosen, axis=0)  8.21 us
    all_to_all x1, starting transfers between devices, body(): lax.all_to_all(request_list, ('gx', 'gy'), split_axis=0, concat_axis=0, t...  7.33 us
    all_to_all x1, waiting for transfers between devices, body(): lax.all_to_all(exitant_radiance[2].astype(jnp.bfloat16), ('gx', 'gy'), sp...  7.05 us
  transfers between devices with their start and end apart: 6, of which 4 were waited for; matrix products, arithmetic and copies ran while one was open for 40% of the time, Pallas kernels for 0%

commit v1 on v0

v1 whole, which is shorter than its diff:
```python
import functools

import jax
import jax.numpy as jnp
from jax import lax
from jax.experimental import pallas as pl
from jax.experimental.pallas import tpu as pltpu
from jax.sharding import PartitionSpec as P

COLORS = 3
NEAR = 16
CAP = 2
AXES = ("gx", "gy")
VMEM_LIMIT = 48 * 1024 * 1024


def split3(f):
    hi = f.astype(jnp.bfloat16).astype(jnp.float32)
    rest = f - hi
    mid = rest.astype(jnp.bfloat16).astype(jnp.float32)
    return hi, mid, rest - mid


def source_features(pos, nrm, area):
    lanes = pos.shape[1]
    m = nrm * (area * (1.0 / jnp.pi))
    sq = jnp.sum(pos * pos, axis=0, keepdims=True)
    d = -jnp.sum(m * pos, axis=0, keepdims=True)
    feat = jnp.concatenate([pos, sq, m, d], axis=0)
    hi, mid, lo = split3(feat)
    ones = jnp.ones((8, lanes), jnp.float32)
    half = jnp.concatenate([hi, hi, hi, mid, mid, lo, ones, jnp.zeros_like(ones)], axis=0)
    return jnp.concatenate([half, half], axis=0).T


def receiver_weights(pos, nrm):
    lanes = pos.shape[1]
    zero3 = jnp.zeros((3, lanes), jnp.float32)
    zero1 = jnp.zeros((1, lanes), jnp.float32)
    one1 = jnp.ones((1, lanes), jnp.float32)
    zero5 = jnp.zeros((5, lanes), jnp.float32)
    zero8 = jnp.zeros((8, lanes), jnp.float32)

    def column(feat, const):
        hi, mid, lo = split3(feat)
        chi, cmid, clo = split3(const)
        return jnp.concatenate(
            [hi, mid, lo, hi, mid, hi, jnp.concatenate([chi, cmid, clo, zero5], axis=0), zero8],
            axis=0,
        )

    dist = column(
        jnp.concatenate([-2.0 * pos, one1, zero3, zero1], axis=0),
        jnp.sum(pos * pos, axis=0, keepdims=True) + 1.0,
    )
    along_p = column(
        jnp.concatenate([nrm, zero1, zero3, zero1], axis=0),
        -jnp.sum(nrm * pos, axis=0, keepdims=True),
    )
    along_q = column(jnp.concatenate([zero3, zero1, pos, one1], axis=0), zero1)
    return jnp.concatenate([dist, along_p, along_q], axis=1)


def fill_tables(geom, count, even, odd):
    def one(t, carry):
        rows = source_features(*geom(t))
        lane = lax.broadcasted_iota(jnp.int32, rows.shape, 1)
        even[t] = jnp.where(lane < 64, rows, 0.0).astype(jnp.bfloat16)
        odd[t] = jnp.where(lane < 64, 0.0, rows).astype(jnp.bfloat16)
        return carry

    lax.fori_loop(0, count, one, 0)


def row_tiles(rows_ref, slot, count, weights, even, odd, table, lhs, tiles):
    v = tiles.shape[-1]

    def four(i, carry):
        t = [rows_ref[slot, i * 4 + j] for j in range(4)]
        x = jnp.concatenate([even[t[0]] + odd[t[1]], even[t[2]] + odd[t[3]]], axis=0)
        g = jnp.dot(x, weights, preferred_element_type=jnp.float32)
        for j in range(4):
            r, c = (j // 2) * v, (j % 2) * 3 * v
            dist = g[r : r + v, c : c + v]
            ap = g[r : r + v, c + v : c + 2 * v]
            aq = g[r : r + v, c + 2 * v : c + 3 * v]
            f = jnp.maximum(ap, 0.0) * jnp.maximum(aq, 0.0) / (dist * dist)
            at = pl.multiple_of((i * 4 + j) * v, v)
            tiles[0, pl.ds(at, v), :] = f.astype(jnp.bfloat16)
            lhs[:, pl.ds(at, v)] = table[t[j], 0 : lhs.shape[0], :]
        return carry

    lax.fori_loop(0, count // 4, four, 0)


def gather_rows(rows_ref, slot, count, table, lhs, v):
    for j in range(count):
        lhs[:, j * v : (j + 1) * v] = table[rows_ref[slot, j], 0 : lhs.shape[0], :]


def block_diag(w):
    z = jnp.zeros_like(w)
    return jnp.concatenate(
        [jnp.concatenate([w, z], axis=1), jnp.concatenate([z, w], axis=1)], axis=0
    ).astype(jnp.bfloat16)


def albedo_rows(alb, rows, per_color):
    r = lax.broadcasted_iota(jnp.int32, (rows, alb.shape[1]), 0)
    out = jnp.broadcast_to(alb[COLORS - 1 : COLORS, :], (rows, alb.shape[1]))
    for c in range(COLORS - 2, -1, -1):
        out = jnp.where(r < (c + 1) * per_color, alb[c : c + 1, :], out)
    return out


def near_kernel(rows_ref, pos, nrm, area, table, tiles, acc, even, odd, lhs):
    s = pl.program_id(0)

    @pl.when(s == 0)
    def _():
        fill_tables(lambda t: (pos[t], nrm[t], area[t]), even.shape[0], even, odd)

    weights = block_diag(receiver_weights(pos[s], nrm[s]))
    row_tiles(rows_ref, s, rows_ref.shape[1], weights, even, odd, table, lhs, tiles)
    acc[0] = jnp.dot(lhs[...], tiles[0], preferred_element_type=jnp.float32)


def finish(total, s, alb, area, ch, out, energy):
    val = total * albedo_rows(alb, total.shape[0], ch // COLORS)
    r = lax.broadcasted_iota(jnp.int32, val.shape, 0)
    part = jnp.sum(jnp.where(r < ch, val * val * area, 0.0), axis=0, keepdims=True)
    energy[...] = jnp.where(s == 0, part, energy[...] + part)
    return val.astype(jnp.bfloat16)


def far_kernel(
    ch, rows_ref, pos, nrm, area, alb, near_acc, table, tiles, out, energy, even, odd, lhs
):
    s = pl.program_id(0)

    def geom(t):
        g = table[t, ch:, :].astype(jnp.float32)
        return g[0:3] + g[3:6], g[6:9] + g[9:12], g[12:13]

    @pl.when(s == 0)
    def _():
        fill_tables(geom, even.shape[0], even, odd)

    weights = block_diag(receiver_weights(pos[s], nrm[s]))
    row_tiles(rows_ref, s, rows_ref.shape[1], weights, even, odd, table, lhs, tiles)
    total = near_acc[0] + jnp.dot(lhs[...], tiles[0], preferred_element_type=jnp.float32)
    out[0] = finish(total, s, alb[s], area[s], ch, out, energy)


def near_second(rows_ref, table, tiles, acc, lhs):
    s = pl.program_id(0)
    gather_rows(rows_ref, s, rows_ref.shape[1], table, lhs, tiles.shape[-1])
    acc[0] = jnp.dot(lhs[...], tiles[0], preferred_element_type=jnp.float32)


def far_second(ch, rows_ref, area, alb, near_acc, table, tiles, out, energy, lhs):
    s = pl.program_id(0)
    gather_rows(rows_ref, s, rows_ref.shape[1], table, lhs, tiles.shape[-1])
    total = near_acc[0] + jnp.dot(lhs[...], tiles[0], preferred_element_type=jnp.float32)
    out[0] = finish(total, s, alb[s], area[s], ch, out, energy)[0:ch]


def whole(x):
    nd = len(x.shape)
    return pl.BlockSpec(x.shape, lambda s: (0,) * nd)


def per_slot(shape):
    nd = len(shape)
    return pl.BlockSpec((1,) + tuple(shape[1:]), lambda s: (s,) + (0,) * (nd - 1))


def call(kernel, name, ins, sliced, outs, scratch, flops):
    specs = [pl.BlockSpec(memory_space=pltpu.SMEM)]
    for i, x in enumerate(ins[1:], 1):
        specs.append(per_slot(x.shape) if i in sliced else whole(x))
    return pl.pallas_call(
        kernel,
        name=name,
        grid=(ins[0].shape[0],),
        in_specs=specs,
        out_specs=[per_slot(o.shape) if len(o.shape) == 3 else whole(o) for o in outs],
        out_shape=outs,
        scratch_shapes=scratch,
        compiler_params=pltpu.CompilerParams(vmem_limit_bytes=VMEM_LIMIT),
        cost_estimate=pl.CostEstimate(flops=flops, bytes_accessed=1 << 20, transcendentals=0),
    )(*ins)


def body(transfer, positions, normals, area, albedo, pairs, home):
    n = lax.axis_size(AXES)
    me = lax.axis_index(AXES)
    b, ch, v = transfer.shape
    far = pairs.shape[1] - NEAR
    rows = -(-ch // 16) * 16
    bf16, f32 = jnp.bfloat16, jnp.float32

    ids = jnp.arange(home.shape[0], dtype=jnp.int32)
    slot_ids = jnp.sum(jnp.where(pairs[:, :, None] == ids, home, 0), axis=2)
    near_rows = slot_ids[:, :NEAR] - me * b
    far_ids = slot_ids[:, NEAR:]
    owner = far_ids // b
    local = far_ids - owner * b
    devs = jnp.arange(n, dtype=jnp.int32)
    mine = owner[:, :, None] == devs
    low = jnp.min(jnp.where(mine, local[:, :, None], b - 1), axis=(0, 1))
    high = jnp.max(jnp.where(mine, local[:, :, None], 0), axis=(0, 1))
    low_of = jnp.sum(jnp.where(mine, low, 0), axis=2)
    far_rows = owner * CAP + (local > low_of).astype(jnp.int32)
    asked = lax.all_to_all(
        jnp.stack([low, high], axis=1), AXES, split_axis=0, concat_axis=0, tiled=True
    ).reshape(-1)

    def hi_mid(x):
        hi = lax.reduce_precision(x, 8, 7)
        return [hi.astype(bf16), (x - hi).astype(bf16)]

    packed = jnp.concatenate(
        [transfer] + hi_mid(positions) + hi_mid(normals) + [area[:, None, :].astype(bf16)], axis=1
    )
    sent = jnp.take(packed, asked, axis=0)
    arrived = lax.all_to_all(sent, AXES, split_axis=0, concat_axis=0, tiled=True)

    area3 = area[:, None, :]
    lhs = lambda j: pltpu.VMEM((rows, j * v), bf16)
    tab = lambda t: pltpu.VMEM((t, v, v), bf16)
    acc_shape = jax.ShapeDtypeStruct((b, rows, v), f32)
    en_shape = jax.ShapeDtypeStruct((1, v), f32)
    near_tiles, near_acc = call(
        near_kernel, "near_first",
        (near_rows, positions, normals, area3, packed), (),
        [jax.ShapeDtypeStruct((b, NEAR * v, v), bf16), acc_shape],
        [tab(b), tab(b), lhs(NEAR)],
        2 * b * NEAR * v * v * 400,
    )
    far_tiles, one, en_one = call(
        functools.partial(far_kernel, ch), "far_first",
        (far_rows, positions, normals, area3, albedo, near_acc, arrived), (5,),
        [
            jax.ShapeDtypeStruct((b, far * v, v), bf16),
            jax.ShapeDtypeStruct((b, rows, v), bf16),
            en_shape,
        ],
        [tab(n * CAP), tab(n * CAP), lhs(far)],
        2 * b * far * v * v * 400,
    )
    sent2 = jnp.take(one, asked, axis=0)
    arrived2 = lax.all_to_all(sent2, AXES, split_axis=0, concat_axis=0, tiled=True)
    (near2,) = call(
        near_second, "near_second", (near_rows, one, near_tiles), (2,),
        [acc_shape], [lhs(NEAR)], 2 * b * NEAR * v * v * rows,
    )
    two, en_two = call(
        functools.partial(far_second, ch), "far_second",
        (far_rows, area3, albedo, near2, arrived2, far_tiles), (3, 5),
        [jax.ShapeDtypeStruct((b, ch, v), bf16), en_shape],
        [lhs(far)], 2 * b * far * v * v * rows,
    )
    part = jnp.stack([jnp.sum(en_one), jnp.sum(en_two)])
    parts = lax.all_to_all(
        jnp.broadcast_to(part, (n, 2)), AXES, split_axis=0, concat_axis=0, tiled=True
    )
    energies = jnp.sum(parts, axis=0) * (1.0 / (n * b * v * ch))
    return one[:, :ch], two, energies


def solution(mesh):
    return jax.shard_map(
        body,
        mesh=mesh,
        in_specs=(
            P(AXES, None, None),
            P(AXES, None, None),
            P(AXES, None, None),
            P(AXES, None),
            P(AXES, None, None),
            P(AXES, None),
            P(),
        ),
        out_specs=(P(AXES, None, None), P(AXES, None, None), P()),
        check_vma=False,
    )
```

time: 293 us -> 164 us (0.56)
  Pallas kernels: 0 us -> 86.6 us
  local copies, waits for them, and re-layouts: 70.5 us -> 7.16 us
  other arithmetic: 72.8 us -> 11.4 us
  matrix products: 44.8 us -> 0 us
  blocking collectives: 37.9 us -> 0 us
  starting transfers between devices: 29.7 us -> 16.2 us
  waiting for transfers between devices: 29.4 us -> 40.4 us
  loops' own time: 5.89 us -> 0 us
    pallas_call x0 -> x4, Pallas kernels: none -> 86.6 us  [call(): pl.pallas_call(kernel, name=name, grid=(ins[0].shape[0],), in_specs=specs...]
    dynamic_update_slice x8 -> x0, other arithmetic: 52.1 us -> none  [build_tiles(): return lax.map(group_tiles, jnp.arange(turns, dtype=jnp.int32))]
    dot_general x16 -> x0, matrix products: 44.8 us -> none  [group_term(): jnp.einsum('wxmy,wxsy->wms', collected_values, transfer_factors, preferre...]
    gather x49 -> x2, local copies, waits for them, and re-layouts: 45.2 us -> 1.65 us  [the longest x1 0.84 us: body(): sent = jnp.take(packed, asked, axis=0)]
    psum x1 -> x0, blocking collectives: 37.9 us -> none  [total_energy(): return lax.psum(local_part, ('gx', 'gy'))]
    all_to_all x6 -> x4, starting transfers between devices: 29.7 us -> 16.2 us  [the longest x1 7.33 us: body(): lax.all_to_all(jnp.stack([low, high], axis=1), AXES, split_axis=0, concat...]
    all_to_all x6 -> x4, waiting for transfers between devices: 29.4 us -> 40.4 us  [the longest x1 21.4 us: body(): lax.all_to_all(sent2, AXES, split_axis=0, concat_axis=0, tiled=True)]
    dynamic_update_slice x16 -> x0, local copies, waits for them, and re-layouts: 6.7 us -> none  [apply_tiles(): summed = lax.map(group_term, (grouped_rows, tiles))]
  transfers between devices with their start and end apart: 6 -> 4, of which waited for: 4 -> 4; matrix products, arithmetic and copies ran while one was open for 40% -> 5% of each run, Pallas kernels for 0% -> 22%
where the time goes in v1:
time: 164 us; the launch traced here: 163 us
  Pallas kernels  86.6 us (53%)
  waiting for transfers between devices  40.4 us (25%)
  starting transfers between devices  16.2 us (10%)
  other arithmetic  11.4 us (7%)
  local copies, waits for them, and re-layouts  7.16 us (4%)
    pallas_call x4, Pallas kernels, call(): pl.pallas_call(kernel, name=name, grid=(ins[0].shape[0],), in_specs=specs...  86.6 us
    all_to_all x1, waiting for transfers between devices, body(): lax.all_to_all(sent2, AXES, split_axis=0, concat_axis=0, tiled=True)  21.4 us
    all_to_all x1, waiting for transfers between devices, body(): lax.all_to_all(sent, AXES, split_axis=0, concat_axis=0, tiled=True)  11.3 us
    all_to_all x1, starting transfers between devices, body(): lax.all_to_all(jnp.stack([low, high], axis=1), AXES, split_axis=0, concat...  7.33 us
    all_to_all x1, waiting for transfers between devices, body(): lax.all_to_all(jnp.broadcast_to(part, (n, 2)), AXES, split_axis=0, concat...  5.54 us
    all_to_all x1, starting transfers between devices, body(): lax.all_to_all(sent, AXES, split_axis=0, concat_axis=0, tiled=True)  3.68 us
  transfers between devices with their start and end apart: 4, of which 4 were waited for; matrix products, arithmetic and copies ran while one was open for 5% of the time, Pallas kernels for 22%

profile of v1, /device:TPU:0, one launch (start us, length us, event | category | flops | bytes accessed | tf_op | source)
XLA Modules:
  0.0 162.6 jit_solution(10010082679043004565)
XLA Ops:
  0.6 1.2 select_reduce_fusion
  1.8 0.1 add_select_fusion
  1.9 0.2 select_reduce_fusion.1
  2.1 0.7 copy.97
  2.8 7.3 %all-to-all-start = ((s32[32,1,2]{2,1,0:T(1,128)}), s32[32,1,2]{2,1,0:T(1,128)S(1)}, u32[]{:S(2)}, u32[]{:S(2)}) async-start(s32[32,1,2]{2,1,0:T(1,128)} %copy.97), calls=%async_computation | async-start | bytes 32768 | tf_op jit(solution)/shard_map/all_to_all | solution.py:215
  10.1 0.7 reduce_precision.6
  10.9 0.7 reduce_precision.7
  11.6 0.8 fusion
  12.4 0.7 convert_bitcast_fusion
  13.2 1.1 copy.93
  14.3 0.8 concatenate.3.table
  15.0 2.2 %all-to-all-done = s32[32,1,2]{2,1,0:T(1,128)S(1)} async-done(((s32[32,1,2]{2,1,0:T(1,128)}), s32[32,1,2]{2,1,0:T(1,128)S(1)}, u32[]{:S(2)}, u32[]{:S(2)}) %all-to-all-start) | async-done | bytes 288 | tf_op jit(solution)/shard_map/all_to_all | solution.py:215
  17.2 0.1 reshape.58
  17.3 0.5 broadcast.59
  17.9 0.7 reduce.6
  18.5 0.1 reshape.57
  18.7 0.8 gather_fusion
  19.5 1.3 broadcast_select_fusion
  20.8 0.0 copy-start.1
  20.8 0.0 copy-start
  20.8 3.7 %all-to-all-start.1 = ((bf16[64,88,128]{2,1,0:T(8,128)(2,1)}), bf16[64,88,128]{2,1,0:T(8,128)(2,1)S(1)}, u32[]{:S(2)}, u32[]{:S(2)}) async-start(bf16[64,88,128]{2,1,0:T(8,128)(2,1)} %broadcast_select_fusion), calls=%async_computation.1 | async-start | bytes 2883584 | tf_op jit(solution)/shard_map/all_to_all | solution.py:227
  24.5 0.0 copy-done.1
  24.6 0.4 select_reduce_fusion.2
  25.0 0.1 convert_add_fusion.rows_ref
  25.1 0.0 copy-done
  25.1 23.9 %near_first.1 = (bf16[16,2048,128]{2,1,0:T(8,128)(2,1)}, f32[16,80,128]{2,1,0:T(8,128)S(1)}) custom-call(s32[16,16]{1,0:T(8,128)S(1)} %slice_subtract_fusion.rows_ref, f32[16,3,128]{2,1,0:T(4,128)S(1)} %get-tuple-element.40.pos, f32[16,3,128]{2,1,0:T(4,128)S(1)} %get-tuple-element.43.nrm, f32[16,1,128]{2,1,0:T(1,128)S(1)} %bitcast.14, ...), custom_call_target="tpu_custom_call" | custom-call | flops 3355443200 | bytes 1048576 | tf_op jit(solution)/shard_map/near_first/pallas_call | solution.py:182
  49.1 11.3 %all-to-all-done.1.table = bf16[64,88,128]{2,1,0:T(8,128)(2,1)S(1)} async-done(((bf16[64,88,128]{2,1,0:T(8,128)(2,1)}), bf16[64,88,128]{2,1,0:T(8,128)(2,1)S(1)}, u32[]{:S(2)}, u32[]{:S(2)}) %all-to-all-start.1) | async-done | bytes 1441824 | tf_op jit(solution)/shard_map/all_to_all | solution.py:227
  60.4 38.7 %far_first.1 = (bf16[16,3072,128]{2,1,0:T(8,128)(2,1)}, bf16[16,80,128]{2,1,0:T(8,128)(2,1)S(1)}, f32[1,128]{1,0:T(1,128)S(1)}) custom-call(s32[16,24]{1,0:T(8,128)S(1)} %convert_add_fusion.rows_ref, f32[16,3,128]{2,1,0:T(4,128)S(1)} %get-tuple-element.40.pos, f32[16,3,128]{2,1,0:T(4,128)S(1)} %get-tuple-element.43.nrm, f32[16,1,128]{2,1,0:T(1,128)S(1)} %bitcast.15, ...), custom_call_target="tpu_custom_call" | custom-call | flops 5033164800 | bytes 1048576 | tf_op jit(solution)/shard_map/far_first/pallas_call | solution.py:182
  99.1 0.8 gather_fusion.1
  100.0 1.2 broadcast_select_fusion.1
  101.2 2.7 %all-to-all-start.2 = ((bf16[64,80,128]{2,1,0:T(8,128)(2,1)}), bf16[64,80,128]{2,1,0:T(8,128)(2,1)S(1)}, u32[]{:S(2)}, u32[]{:S(2)}) async-start(bf16[64,80,128]{2,1,0:T(8,128)(2,1)} %broadcast_select_fusion.1), calls=%async_computation.2 | async-start | bytes 2621440 | tf_op jit(solution)/shard_map/all_to_all | solution.py:253
  103.9 0.6 reduce_sum.47
  104.5 11.1 %near_second.1.near_acc = f32[16,80,128]{2,1,0:T(8,128)S(1)} custom-call(s32[16,16]{1,0:T(8,128)S(1)} %slice_subtract_fusion.rows_ref, bf16[16,80,128]{2,1,0:T(8,128)(2,1)S(1)} %get-tuple-element.11.table, bf16[16,2048,128]{2,1,0:T(8,128)(2,1)} %get-tuple-element.12.tiles), custom_call_target="tpu_custom_call" | custom-call | flops 671088640 | bytes 1048576 | tf_op jit(solution)/shard_map/near_second/pallas_call | solution.py:182
  115.6 21.4 %all-to-all-done.2.table = bf16[64,80,128]{2,1,0:T(8,128)(2,1)S(1)} async-done(((bf16[64,80,128]{2,1,0:T(8,128)(2,1)}), bf16[64,80,128]{2,1,0:T(8,128)(2,1)S(1)}, u32[]{:S(2)}, u32[]{:S(2)}) %all-to-all-start.2) | async-done | bytes 1310752 | tf_op jit(solution)/shard_map/all_to_all | solution.py:253
  137.0 12.8 %far_second.1 = (bf16[16,75,128]{2,1,0:T(8,128)(2,1)S(1)}, f32[1,128]{1,0:T(1,128)S(1)}) custom-call(s32[16,24]{1,0:T(8,128)S(1)} %convert_add_fusion.rows_ref, f32[16,1,128]{2,1,0:T(1,128)S(1)} %bitcast.16, f32[16,3,128]{2,1,0:T(4,128)S(1)} %copy.100.alb, f32[16,80,128]{2,1,0:T(8,128)S(1)} %near_second.1.near_acc, ...), custom_call_target="tpu_custom_call" | custom-call | flops 1006632960 | bytes 1048576 | tf_op jit(solution)/shard_map/far_second/pallas_call | solution.py:182
  149.8 0.6 reduce_sum.48
  150.4 1.4 pad_maximum_fusion
  151.7 0.6 broadcast_in_dim.76
  152.3 2.6 %all-to-all-start.3 = ((f32[32,1,2]{2,1,0:T(1,128)}), f32[32,1,2]{2,1,0:T(1,128)S(1)}, u32[]{:S(2)}, u32[]{:S(2)}) async-start(f32[32,1,2]{2,1,0:T(1,128)} %broadcast_in_dim.76), calls=%async_computation.3 | async-start | bytes 32768 | tf_op jit(solution)/shard_map/all_to_all | solution.py:265
  154.9 0.8 copy.103
  155.7 0.8 copy.104
  156.5 5.5 %all-to-all-done.3 = f32[32,1,2]{2,1,0:T(1,128)S(1)} async-done(((f32[32,1,2]{2,1,0:T(1,128)}), f32[32,1,2]{2,1,0:T(1,128)S(1)}, u32[]{:S(2)}, u32[]{:S(2)}) %all-to-all-start.3) | async-done | bytes 288 | tf_op jit(solution)/shard_map/all_to_all | solution.py:265
  162.1 0.1 reduce_sum.49
  162.1 0.5 broadcast_multiply_fusion
  (9 shorter events, 0.1 us)
Async XLA Ops:
  2.8 14.4 %all-to-all-start = ((s32[32,1,2]{2,1,0:T(1,128)}), s32[32,1,2]{2,1,0:T(1,128)S(1)}, u32[]{:S(2)}, u32[]{:S(2)}) async-start(s32[32,1,2]{2,1,0:T(1,128)} %copy.97), calls=%async_computation | async-start | bytes 32768 | tf_op jit(solution)/shard_map/all_to_all | solution.py:215
  20.8 3.7 %copy-start.1 = (f32[16,3,128]{2,0,1:T(8,128)S(1)}, f32[16,3,128]{2,0,1:T(8,128)}, u32[]{:S(2)}) copy-start(f32[16,3,128]{2,0,1:T(8,128)} %param.11) | copy-start | bytes 73732
  20.8 4.3 %copy-start = (f32[16,128]{1,0:T(8,128)S(1)}, f32[16,128]{1,0:T(8,128)}, u32[]{:S(2)}) copy-start(f32[16,128]{1,0:T(8,128)} %param.10) | copy-start | bytes 24580
  20.8 39.6 %all-to-all-start.1 = ((bf16[64,88,128]{2,1,0:T(8,128)(2,1)}), bf16[64,88,128]{2,1,0:T(8,128)(2,1)S(1)}, u32[]{:S(2)}, u32[]{:S(2)}) async-start(bf16[64,88,128]{2,1,0:T(8,128)(2,1)} %broadcast_select_fusion), calls=%async_computation.1 | async-start | bytes 2883584 | tf_op jit(solution)/shard_map/all_to_all | solution.py:227
  101.2 35.8 %all-to-all-start.2 = ((bf16[64,80,128]{2,1,0:T(8,128)(2,1)}), bf16[64,80,128]{2,1,0:T(8,128)(2,1)S(1)}, u32[]{:S(2)}, u32[]{:S(2)}) async-start(bf16[64,80,128]{2,1,0:T(8,128)(2,1)} %broadcast_select_fusion.1), calls=%async_computation.2 | async-start | bytes 2621440 | tf_op jit(solution)/shard_map/all_to_all | solution.py:253
  152.3 9.7 %all-to-all-start.3 = ((f32[32,1,2]{2,1,0:T(1,128)}), f32[32,1,2]{2,1,0:T(1,128)S(1)}, u32[]{:S(2)}, u32[]{:S(2)}) async-start(f32[32,1,2]{2,1,0:T(1,128)} %broadcast_in_dim.76), calls=%async_computation.3 | async-start | bytes 32768 | tf_op jit(solution)/shard_map/all_to_all | solution.py:265

commit v2 on v1

v2 whole, which is shorter than its diff:
```python
import functools

import jax
import jax.numpy as jnp
from jax import lax
from jax.experimental import pallas as pl
from jax.experimental.pallas import tpu as pltpu
from jax.sharding import PartitionSpec as P

COLORS = 3
NEAR = 16
CAP = 2
AXES = ("gx", "gy")
GEO = 16
VMEM_LIMIT = 62 * 1024 * 1024
MESH = pl.DeviceIdType.MESH


def split3(f):
    hi = f.astype(jnp.bfloat16).astype(jnp.float32)
    rest = f - hi
    mid = rest.astype(jnp.bfloat16).astype(jnp.float32)
    return hi, mid, rest - mid


def source_features(pos, nrm, area):
    lanes = pos.shape[1]
    m = nrm * (area * (1.0 / jnp.pi))
    sq = jnp.sum(pos * pos, axis=0, keepdims=True)
    d = -jnp.sum(m * pos, axis=0, keepdims=True)
    feat = jnp.concatenate([pos, sq, m, d], axis=0)
    hi, mid, lo = split3(feat)
    ones = jnp.ones((8, lanes), jnp.float32)
    half = jnp.concatenate([hi, hi, hi, mid, mid, lo, ones, jnp.zeros_like(ones)], axis=0)
    return jnp.concatenate([half, half], axis=0).T


def receiver_weights(pos, nrm):
    lanes = pos.shape[1]
    zero3 = jnp.zeros((3, lanes), jnp.float32)
    zero1 = jnp.zeros((1, lanes), jnp.float32)
    one1 = jnp.ones((1, lanes), jnp.float32)
    zero5 = jnp.zeros((5, lanes), jnp.float32)
    zero8 = jnp.zeros((8, lanes), jnp.float32)

    def column(feat, const):
        hi, mid, lo = split3(feat)
        chi, cmid, clo = split3(const)
        return jnp.concatenate(
            [hi, mid, lo, hi, mid, hi, jnp.concatenate([chi, cmid, clo, zero5], axis=0), zero8],
            axis=0,
        )

    dist = column(
        jnp.concatenate([-2.0 * pos, one1, zero3, zero1], axis=0),
        jnp.sum(pos * pos, axis=0, keepdims=True) + 1.0,
    )
    along_p = column(
        jnp.concatenate([nrm, zero1, zero3, zero1], axis=0),
        -jnp.sum(nrm * pos, axis=0, keepdims=True),
    )
    along_q = column(jnp.concatenate([zero3, zero1, pos, one1], axis=0), zero1)
    return jnp.concatenate([dist, along_p, along_q], axis=1)


def block_diag(w):
    z = jnp.zeros_like(w)
    return jnp.concatenate(
        [jnp.concatenate([w, z], axis=1), jnp.concatenate([z, w], axis=1)], axis=0
    ).astype(jnp.bfloat16)


def albedo_rows(alb, rows, per_color):
    r = lax.broadcasted_iota(jnp.int32, (rows, alb.shape[1]), 0)
    out = jnp.broadcast_to(alb[COLORS - 1 : COLORS, :], (rows, alb.shape[1]))
    for c in range(COLORS - 2, -1, -1):
        out = jnp.where(r < (c + 1) * per_color, alb[c : c + 1, :], out)
    return out


def fill_table(geom, count, feats):
    def one(t, carry):
        feats[t] = source_features(*geom(t)).astype(jnp.bfloat16)
        return carry

    lax.fori_loop(0, count, one, 0)


def row_tiles(rows_ref, slot, base, weights, feats, tiles):
    v = tiles.shape[-1]
    first = lax.broadcasted_iota(jnp.int32, (v, v), 1) < v // 2
    for i in range(rows_ref.shape[1] // 4):
        t = [rows_ref[slot, i * 4 + j] for j in range(4)]
        x = jnp.concatenate(
            [
                jnp.where(first, feats[t[0]], feats[t[1]]),
                jnp.where(first, feats[t[2]], feats[t[3]]),
            ],
            axis=0,
        )
        g = jnp.dot(x, weights, preferred_element_type=jnp.float32)
        for j in range(4):
            r, c = (j // 2) * v, (j % 2) * 3 * v
            dist = g[r : r + v, c : c + v]
            ap = g[r : r + v, c + v : c + 2 * v]
            aq = g[r : r + v, c + 2 * v : c + 3 * v]
            f = jnp.maximum(ap, 0.0) * jnp.maximum(aq, 0.0) / (dist * dist)
            at = base + (i * 4 + j) * v
            tiles[slot, at : at + v, :] = f.astype(jnp.bfloat16)


def contract(rows_ref, slot, base, load, lhs, tiles):
    v = tiles.shape[-1]
    count = rows_ref.shape[1]
    for j in range(count):
        lhs[:, j * v : (j + 1) * v] = load(rows_ref[slot, j])
    return jnp.dot(
        lhs[:, 0 : count * v],
        tiles[slot, base : base + count * v, :],
        preferred_element_type=jnp.float32,
    )


def bounce_kernel(
    n, ny,
    near_rows, far_rows, asked,
    transfer, pos, nrm, area, alb,
    one_ref, two_ref, energy_ref,
    local, geo_local, geo_out, geo_in, box_out, box_in, box_in2,
    near_feats, far_feats, tiles, lhs, acc, one, en, en_in,
    gs, gr, rs, rr, ss, sr, e1s, e1r, e2s, e2r,
):
    bf16, f32 = jnp.bfloat16, jnp.float32
    me = lax.axis_index("gx") * ny + lax.axis_index("gy")
    b, ch, v = transfer.shape
    rows = local.shape[1]
    near = near_rows.shape[1]

    def peer(d):
        t = lax.rem(me + d, n)
        return t, (t // ny, lax.rem(t, ny))

    def each_peer(fn):
        def step(d, carry):
            fn(d)
            return carry

        lax.fori_loop(1, n, step, 0)

    def copies(src, dst, send, recv):
        def make(d):
            t, dev = peer(d)
            return pltpu.make_async_remote_copy(
                src_ref=src(t), dst_ref=dst, send_sem=send.at[d], recv_sem=recv.at[d],
                device_id=dev, device_id_type=MESH,
            )

        return make

    def pair(ref, t):
        return ref.at[pl.ds(t * CAP, CAP)]

    geo_cp = copies(lambda t: pair(geo_out, t), pair(geo_in, me), gs, gr)
    rad_cp = copies(lambda t: pair(box_out, t), pair(box_in, me), rs, rr)
    sec_cp = copies(lambda t: pair(box_out, t), pair(box_in2, me), ss, sr)
    e1_cp = copies(lambda t: en.at[0], en_in.at[0, me], e1s, e1r)
    e2_cp = copies(lambda t: en.at[1], en_in.at[1, me], e2s, e2r)

    barrier = pltpu.get_barrier_semaphore()
    each_peer(lambda d: pl.semaphore_signal(barrier, inc=1, device_id=peer(d)[1], device_id_type=MESH))

    def stage(t, carry):
        local[t] = jnp.concatenate(
            [transfer[t], jnp.zeros((rows - ch, v), bf16)], axis=0
        )
        p_hi, p_mid, _ = split3(pos[t])
        n_hi, n_mid, _ = split3(nrm[t])
        geo_local[t] = jnp.concatenate(
            [p_hi, p_mid, n_hi, n_mid, area[t], jnp.zeros((GEO - 13, v), f32)], axis=0
        ).astype(bf16)
        return carry

    lax.fori_loop(0, b, stage, 0)

    def pack(source, out):
        def step(t, carry):
            for k in range(CAP):
                out[t * CAP + k] = source[asked[t * CAP + k]]
            return carry

        lax.fori_loop(0, n, step, 0)

    pack(geo_local, geo_out)
    pack(local, box_out)
    for box in (geo_in, box_in, box_in2):
        for k in range(CAP):
            box[me * CAP + k] = jnp.zeros(box.shape[1:], bf16)
    pl.semaphore_wait(barrier, n - 1)
    each_peer(lambda d: geo_cp(d).start())
    each_peer(lambda d: rad_cp(d).start())

    def weights_of(s):
        return block_diag(receiver_weights(pos[s], nrm[s]))

    fill_table(lambda t: (pos[t], nrm[t], area[t]), b, near_feats)

    def near_slot(s, carry):
        row_tiles(near_rows, s, 0, weights_of(s), near_feats, tiles)
        acc[s] = contract(near_rows, s, 0, lambda t: local[t], lhs, tiles)
        return carry

    lax.fori_loop(0, b, near_slot, 0)
    each_peer(lambda d: geo_cp(d).wait())

    def far_geom(t):
        g = geo_in[t].astype(f32)
        return g[0:3] + g[3:6], g[6:9] + g[9:12], g[12:13]

    fill_table(far_geom, n * CAP, far_feats)

    def far_slot(s, carry):
        row_tiles(far_rows, s, near * v, weights_of(s), far_feats, tiles)
        return carry

    lax.fori_loop(0, b, far_slot, 0)
    each_peer(lambda d: rad_cp(d).wait())

    def finish(s, box, e):
        total = acc[s] + contract(far_rows, s, near * v, lambda t: box[t], lhs, tiles)
        val = total * albedo_rows(alb[s], rows, ch // COLORS)
        r = lax.broadcasted_iota(jnp.int32, val.shape, 0)
        part = jnp.sum(jnp.where(r < ch, val * val * area[s], 0.0), axis=0, keepdims=True)
        return val.astype(bf16), e + part

    def first_slot(s, e):
        val, e = finish(s, box_in, e)
        one[s] = val
        one_ref[s] = val[0:ch]
        return e

    zero = jnp.zeros((1, v), f32)
    row0 = lax.broadcasted_iota(jnp.int32, (8, v), 0) == 0
    e1 = lax.fori_loop(0, b, first_slot, zero)
    pack(one, box_out)
    each_peer(lambda d: sec_cp(d).start())
    en[0] = jnp.where(row0, e1, 0.0)
    en_in[0, me] = en[0]

    def near_again(s, carry):
        acc[s] = contract(near_rows, s, 0, lambda t: one[t], lhs, tiles)
        return carry

    lax.fori_loop(0, b, near_again, 0)
    each_peer(lambda d: e1_cp(d).start())
    each_peer(lambda d: sec_cp(d).wait())

    def second_slot(s, e):
        val, e = finish(s, box_in2, e)
        two_ref[s] = val[0:ch]
        return e

    e2 = lax.fori_loop(0, b, second_slot, zero)
    en[1] = jnp.where(row0, e2, 0.0)
    en_in[1, me] = en[1]
    each_peer(lambda d: e2_cp(d).start())
    each_peer(lambda d: e1_cp(d).wait())
    each_peer(lambda d: e2_cp(d).wait())
    energy_ref[...] = jnp.sum(en_in[...], axis=1)


def body(transfer, positions, normals, area, albedo, pairs, home):
    n = lax.axis_size(AXES)
    me = lax.axis_index(AXES)
    b, ch, v = transfer.shape
    far = pairs.shape[1] - NEAR
    rows = -(-ch // 16) * 16
    bf16, f32 = jnp.bfloat16, jnp.float32

    ids = jnp.arange(home.shape[0], dtype=jnp.int32)
    slot_ids = jnp.sum(jnp.where(pairs[:, :, None] == ids, home, 0), axis=2)
    near_rows = slot_ids[:, :NEAR] - me * b
    far_ids = slot_ids[:, NEAR:]
    owner = far_ids // b
    here = far_ids - owner * b
    devs = jnp.arange(n, dtype=jnp.int32)
    mine = owner[:, :, None] == devs
    low = jnp.min(jnp.where(mine, here[:, :, None], b - 1), axis=(0, 1))
    high = jnp.max(jnp.where(mine, here[:, :, None], 0), axis=(0, 1))
    low_of = jnp.sum(jnp.where(mine, low, 0), axis=2)
    far_rows = owner * CAP + (here > low_of).astype(jnp.int32)
    asked = lax.all_to_all(
        jnp.stack([low, high], axis=1), AXES, split_axis=0, concat_axis=0, tiled=True
    ).reshape(-1)

    vmem = pl.BlockSpec(memory_space=pltpu.VMEM)
    smem = pl.BlockSpec(memory_space=pltpu.SMEM)
    sem = pltpu.SemaphoreType.DMA((n,))
    one, two, energy = pl.pallas_call(
        functools.partial(bounce_kernel, n, lax.axis_size("gy")),
        name="bounces",
        in_specs=[smem] * 3 + [vmem] * 5,
        out_specs=[vmem] * 3,
        out_shape=[
            jax.ShapeDtypeStruct((b, ch, v), bf16),
            jax.ShapeDtypeStruct((b, ch, v), bf16),
            jax.ShapeDtypeStruct((2, 8, v), f32),
        ],
        scratch_shapes=[
            pltpu.VMEM((b, rows, v), bf16),
            pltpu.VMEM((b, GEO, v), bf16),
            pltpu.VMEM((n * CAP, GEO, v), bf16),
            pltpu.VMEM((n * CAP, GEO, v), bf16),
            pltpu.VMEM((n * CAP, rows, v), bf16),
            pltpu.VMEM((n * CAP, rows, v), bf16),
            pltpu.VMEM((n * CAP, rows, v), bf16),
            pltpu.VMEM((b, v, v), bf16),
            pltpu.VMEM((n * CAP, v, v), bf16),
            pltpu.VMEM((b, (NEAR + far) * v, v), bf16),
            pltpu.VMEM((rows, far * v), bf16),
            pltpu.VMEM((b, rows, v), f32),
            pltpu.VMEM((b, rows, v), bf16),
            pltpu.VMEM((2, 8, v), f32),
            pltpu.VMEM((2, n, 8, v), f32),
        ]
        + [sem] * 10,
        compiler_params=pltpu.CompilerParams(
            collective_id=0, has_side_effects=True, vmem_limit_bytes=VMEM_LIMIT
        ),
    )(near_rows, far_rows, asked, transfer, positions, normals, area[:, None, :], albedo)
    energies = jnp.sum(energy, axis=(1, 2)) * (1.0 / (n * b * v * ch))
    return one, two, energies


def solution(mesh):
    return jax.shard_map(
        body,
        mesh=mesh,
        in_specs=(
            P(AXES, None, None),
            P(AXES, None, None),
            P(AXES, None, None),
            P(AXES, None),
            P(AXES, None, None),
            P(AXES, None),
            P(),
        ),
        out_specs=(P(AXES, None, None), P(AXES, None, None), P()),
        check_vma=False,
    )
```

time: 164 us -> 116 us (0.71)
  waiting for transfers between devices: 40.4 us -> 1.24 us
  starting transfers between devices: 16.2 us -> 7.33 us
  Pallas kernels: 86.6 us -> 93.5 us
  other arithmetic: 11.4 us -> 4.54 us
    all_to_all x3 -> x0, waiting for transfers between devices: 38.3 us -> none  [the longest x1 21.4 us: body(): lax.all_to_all(sent2, AXES, split_axis=0, concat_axis=0, tiled=True)]
    all_to_all x3 -> x0, starting transfers between devices: 8.91 us -> none  [the longest x1 3.68 us: body(): lax.all_to_all(sent, AXES, split_axis=0, concat_axis=0, tiled=True)]
    pallas_call x4 -> x1, Pallas kernels: 86.6 us -> 93.5 us  [body(): pl.pallas_call(functools.partial(bounce_kernel, n, lax.axis_size('gy')),...]
    unnamed x8 -> x14, local copies, waits for them, and re-layouts: 2.67 us -> 6.78 us
    select_n x3 -> x0, other arithmetic: 2.57 us -> none  [the longest x2 1.33 us: body(): sent = jnp.take(packed, asked, axis=0)]
    gather x2 -> x0, local copies, waits for them, and re-layouts: 1.65 us -> none  [the longest x1 0.84 us: body(): sent = jnp.take(packed, asked, axis=0)]
  transfers between devices with their start and end apart: 4 -> 1, of which waited for: 4 -> 1; matrix products, arithmetic and copies ran while one was open for 5% -> 5% of each run, Pallas kernels for 22% -> 0%
where the time goes in v2:
time: 116 us
  Pallas kernels  93.5 us (81%)
  local copies, waits for them, and re-layouts  8.6 us (7%)
  starting transfers between devices  7.33 us (6%)
  other arithmetic  4.54 us (4%)
  waiting for transfers between devices  1.24 us (1%)
    pallas_call x1, Pallas kernels, body(): pl.pallas_call(functools.partial(bounce_kernel, n, lax.axis_size('gy')),...  93.5 us
    all_to_all x1, starting transfers between devices, body(): lax.all_to_all(jnp.stack([low, high], axis=1), AXES, split_axis=0, concat...  7.33 us
    unnamed x14, local copies, waits for them, and re-layouts  6.78 us
  transfers between devices with their start and end apart: 1, of which 1 were waited for; matrix products, arithmetic and copies ran while one was open for 5% of the time, Pallas kernels for 0%

profile of v2, /device:TPU:0, one launch (start us, length us, event | category | flops | bytes accessed | tf_op | source)
XLA Modules:
  0.0 115.9 jit_solution(15818965529144788799)
XLA Ops:
  0.6 0.0 copy-start.2
  0.6 0.0 copy-start.1
  0.7 1.2 %select_reduce_fusion = s32[16,40]{1,0:T(8,128)S(1)} fusion(s32[512]{0:T(512)} %param.13, s32[16,40]{1,0:T(8,128)} %param.12), kind=kLoop, calls=%fused_computation | loop fusion | flops 982400 | bytes 7168 | tf_op jit(solution)/shard_map/reduce_sum | solution.py:280
  1.9 0.1 add_select_fusion
  2.0 0.2 select_reduce_fusion.1
  2.2 0.7 copy.31
  2.9 7.3 %all-to-all-start = ((s32[32,1,2]{2,1,0:T(1,128)}), s32[32,1,2]{2,1,0:T(1,128)S(1)}, u32[]{:S(2)}, u32[]{:S(2)}) async-start(s32[32,1,2]{2,1,0:T(1,128)} %copy.31), calls=%async_computation | async-start | bytes 32768 | tf_op jit(solution)/shard_map/all_to_all | solution.py:291
  10.2 0.4 select_reduce_fusion.2
  10.7 0.7 convert_add_fusion.far_rows
  11.3 0.6 slice_subtract_fusion.near_rows
  11.9 1.4 %copy.33.pos = f32[16,3,128]{2,1,0:T(4,128)} copy(f32[16,3,128]{2,0,1:T(8,128)} %param.8) | data formatting | bytes 49152 | tf_op args[1]
  13.3 1.4 %copy.34.nrm = f32[16,3,128]{2,1,0:T(4,128)} copy(f32[16,3,128]{2,0,1:T(8,128)} %param.9) | data formatting | bytes 49152 | tf_op args[2]
  14.7 0.0 copy-done.2
  14.7 0.6 copy.35.alb
  15.3 0.0 copy-done.1
  15.3 0.8 copy.32.transfer
  16.1 1.2 %all-to-all-done = s32[32,1,2]{2,1,0:T(1,128)S(1)} async-done(((s32[32,1,2]{2,1,0:T(1,128)}), s32[32,1,2]{2,1,0:T(1,128)S(1)}, u32[]{:S(2)}, u32[]{:S(2)}) %all-to-all-start) | async-done | bytes 288 | tf_op jit(solution)/shard_map/all_to_all | solution.py:291
  17.3 0.5 broadcast.24
  17.9 0.7 reduce.3
  18.5 0.6 reshape.15.asked
  19.2 93.5 %bounces.1 = (bf16[16,75,128]{2,1,0:T(8,128)(2,1)}, bf16[16,75,128]{2,1,0:T(8,128)(2,1)}, f32[2,8,128]{2,1,0:T(8,128)}) custom-call(s32[16,16]{1,0:T(8,128)} %slice_subtract_fusion.near_rows, s32[16,24]{1,0:T(8,128)} %convert_add_fusion.far_rows, s32[64]{0:T(128)} %reshape.15.asked, bf16[16,75,128]{2,1,0:T(8,128)(2,1)} %copy.32.transfer, ...), custom_call_target="tpu_custom_call" | custom-call | tf_op jit(solution)/shard_map/bounces/pallas_call | solution.py:298
  112.7 0.0 copy-start.3
  112.7 0.0 copy-start
  112.7 1.8 %copy.36 = bf16[16,75,128]{2,0,1:T(8,128)(2,1)} copy(bf16[16,75,128]{2,1,0:T(8,128)(2,1)} %get-tuple-element.18) | data formatting | bytes 614400
  114.5 0.0 copy-done.3
  114.5 0.1 reduce_sum.29
  114.6 0.5 broadcast_multiply_fusion
  115.1 0.0 copy-done
  115.1 0.8 copy.37
  (1 shorter events, 0.0 us)
Async XLA Ops:
  0.6 14.0 %copy-start.2 = (f32[16,3,128]{2,0,1:T(8,128)S(1)}, f32[16,3,128]{2,0,1:T(8,128)}, u32[]{:S(2)}) copy-start(f32[16,3,128]{2,0,1:T(8,128)} %param.11) | copy-start | bytes 73732
  0.6 14.7 %copy-start.1 = (bf16[16,75,128]{2,0,1:T(8,128)(2,1)S(1)}, bf16[16,75,128]{2,0,1:T(8,128)(2,1)}, u32[]{:S(2)}) copy-start(bf16[16,75,128]{2,0,1:T(8,128)(2,1)} %param.7) | copy-start | bytes 921604
  2.9 14.5 %all-to-all-start = ((s32[32,1,2]{2,1,0:T(1,128)}), s32[32,1,2]{2,1,0:T(1,128)S(1)}, u32[]{:S(2)}, u32[]{:S(2)}) async-start(s32[32,1,2]{2,1,0:T(1,128)} %copy.31), calls=%async_computation | async-start | bytes 32768 | tf_op jit(solution)/shard_map/all_to_all | solution.py:291
  112.7 1.8 %copy-start.3 = (f32[2,8,128]{2,1,0:T(8,128)S(1)}, f32[2,8,128]{2,1,0:T(8,128)}, u32[]{:S(2)}) copy-start(f32[2,8,128]{2,1,0:T(8,128)} %get-tuple-element.8) | copy-start | bytes 24580
  112.7 2.4 %copy-start = (bf16[16,75,128]{2,1,0:T(8,128)(2,1)S(1)}, bf16[16,75,128]{2,1,0:T(8,128)(2,1)}, u32[]{:S(2)}) copy-start(bf16[16,75,128]{2,1,0:T(8,128)(2,1)} %get-tuple-element.19) | copy-start | bytes 921604

commit v3 on v2

--- a/solution.py
+++ b/solution.py
@@ -109,15 +109,12 @@
             tiles[slot, at : at + v, :] = f.astype(jnp.bfloat16)
 
 
-def contract(rows_ref, slot, base, load, lhs, tiles):
+def contract(rows_ref, slot, base, load, tiles):
     v = tiles.shape[-1]
     count = rows_ref.shape[1]
-    for j in range(count):
-        lhs[:, j * v : (j + 1) * v] = load(rows_ref[slot, j])
+    picked = jnp.concatenate([load(rows_ref[slot, j]) for j in range(count)], axis=1)
     return jnp.dot(
-        lhs[:, 0 : count * v],
-        tiles[slot, base : base + count * v, :],
-        preferred_element_type=jnp.float32,
+        picked, tiles[slot, base : base + count * v, :], preferred_element_type=jnp.float32
     )
 
 
@@ -127,7 +124,7 @@
     transfer, pos, nrm, area, alb,
     one_ref, two_ref, energy_ref,
     local, geo_local, geo_out, geo_in, box_out, box_in, box_in2,
-    near_feats, far_feats, tiles, lhs, acc, one, en, en_in,
+    near_feats, far_feats, tiles, acc, one, en, en_in,
     gs, gr, rs, rr, ss, sr, e1s, e1r, e2s, e2r,
 ):
     bf16, f32 = jnp.bfloat16, jnp.float32
@@ -206,10 +203,17 @@
 
     def near_slot(s, carry):
         row_tiles(near_rows, s, 0, weights_of(s), near_feats, tiles)
-        acc[s] = contract(near_rows, s, 0, lambda t: local[t], lhs, tiles)
         return carry
 
+    def near_sum(table):
+        def step(s, carry):
+            acc[s] = contract(near_rows, s, 0, lambda t: table[t], tiles)
+            return carry
+
+        lax.fori_loop(0, b, step, 0, unroll=2)
+
     lax.fori_loop(0, b, near_slot, 0)
+    near_sum(local)
     each_peer(lambda d: geo_cp(d).wait())
 
     def far_geom(t):
@@ -226,7 +230,7 @@
     each_peer(lambda d: rad_cp(d).wait())
 
     def finish(s, box, e):
-        total = acc[s] + contract(far_rows, s, near * v, lambda t: box[t], lhs, tiles)
+        total = acc[s] + contract(far_rows, s, near * v, lambda t: box[t], tiles)
         val = total * albedo_rows(alb[s], rows, ch // COLORS)
         r = lax.broadcasted_iota(jnp.int32, val.shape, 0)
         part = jnp.sum(jnp.where(r < ch, val * val * area[s], 0.0), axis=0, keepdims=True)
@@ -240,17 +244,13 @@
 
     zero = jnp.zeros((1, v), f32)
     row0 = lax.broadcasted_iota(jnp.int32, (8, v), 0) == 0
-    e1 = lax.fori_loop(0, b, first_slot, zero)
+    e1 = lax.fori_loop(0, b, first_slot, zero, unroll=2)
     pack(one, box_out)
     each_peer(lambda d: sec_cp(d).start())
     en[0] = jnp.where(row0, e1, 0.0)
     en_in[0, me] = en[0]
 
-    def near_again(s, carry):
-        acc[s] = contract(near_rows, s, 0, lambda t: one[t], lhs, tiles)
-        return carry
-
-    lax.fori_loop(0, b, near_again, 0)
+    near_sum(one)
     each_peer(lambda d: e1_cp(d).start())
     each_peer(lambda d: sec_cp(d).wait())
 
@@ -259,7 +259,7 @@
         two_ref[s] = val[0:ch]
         return e
 
-    e2 = lax.fori_loop(0, b, second_slot, zero)
+    e2 = lax.fori_loop(0, b, second_slot, zero, unroll=2)
     en[1] = jnp.where(row0, e2, 0.0)
     en_in[1, me] = en[1]
     each_peer(lambda d: e2_cp(d).start())
@@ -316,7 +316,6 @@
             pltpu.VMEM((b, v, v), bf16),
             pltpu.VMEM((n * CAP, v, v), bf16),
             pltpu.VMEM((b, (NEAR + far) * v, v), bf16),
-            pltpu.VMEM((rows, far * v), bf16),
             pltpu.VMEM((b, rows, v), f32),
             pltpu.VMEM((b, rows, v), bf16),
             pltpu.VMEM((2, 8, v), f32),

time: 116 us -> 113 us (0.974)
  Pallas kernels: 93.5 us -> 89.8 us
    pallas_call x1, Pallas kernels: 93.5 us -> 89.8 us  [body(): pl.pallas_call(functools.partial(bounce_kernel, n, lax.axis_size('gy')),...]
where the time goes in v3:
time: 113 us; the launch traced here: 112 us
  Pallas kernels  89.8 us (79%)
  local copies, waits for them, and re-layouts  8.6 us (8%)
  starting transfers between devices  7.33 us (6%)
  other arithmetic  4.54 us (4%)
  waiting for transfers between devices  1.24 us (1%)
    pallas_call x1, Pallas kernels, body(): pl.pallas_call(functools.partial(bounce_kernel, n, lax.axis_size('gy')),...  89.8 us
    all_to_all x1, starting transfers between devices, body(): lax.all_to_all(jnp.stack([low, high], axis=1), AXES, split_axis=0, concat...  7.33 us
    unnamed x14, local copies, waits for them, and re-layouts  6.78 us
  transfers between devices with their start and end apart: 1, of which 1 were waited for; matrix products, arithmetic and copies ran while one was open for 5% of the time, Pallas kernels for 0%

profile of v3, /device:TPU:0, one launch (start us, length us, event | category | flops | bytes accessed | tf_op | source)
XLA Modules:
  0.0 112.2 jit_solution(10254522770237146731)
XLA Ops:
  0.6 0.0 copy-start.2
  0.6 0.0 copy-start.1
  0.7 1.2 %select_reduce_fusion = s32[16,40]{1,0:T(8,128)S(1)} fusion(s32[512]{0:T(512)} %param.13, s32[16,40]{1,0:T(8,128)} %param.12), kind=kLoop, calls=%fused_computation | loop fusion | flops 982400 | bytes 7168 | tf_op jit(solution)/shard_map/reduce_sum | solution.py:280
  1.9 0.1 add_select_fusion
  2.0 0.2 select_reduce_fusion.1
  2.2 0.7 copy.31
  2.9 7.3 %all-to-all-start = ((s32[32,1,2]{2,1,0:T(1,128)}), s32[32,1,2]{2,1,0:T(1,128)S(1)}, u32[]{:S(2)}, u32[]{:S(2)}) async-start(s32[32,1,2]{2,1,0:T(1,128)} %copy.31), calls=%async_computation | async-start | bytes 32768 | tf_op jit(solution)/shard_map/all_to_all | solution.py:291
  10.2 0.4 select_reduce_fusion.2
  10.7 0.7 convert_add_fusion.far_rows
  11.3 0.6 slice_subtract_fusion.near_rows
  11.9 1.4 %copy.33.pos = f32[16,3,128]{2,1,0:T(4,128)} copy(f32[16,3,128]{2,0,1:T(8,128)} %param.8) | data formatting | bytes 49152 | tf_op args[1]
  13.3 1.4 %copy.34.nrm = f32[16,3,128]{2,1,0:T(4,128)} copy(f32[16,3,128]{2,0,1:T(8,128)} %param.9) | data formatting | bytes 49152 | tf_op args[2]
  14.7 0.0 copy-done.2
  14.7 0.6 copy.35.alb
  15.3 0.0 copy-done.1
  15.3 0.8 copy.32.transfer
  16.1 1.2 %all-to-all-done = s32[32,1,2]{2,1,0:T(1,128)S(1)} async-done(((s32[32,1,2]{2,1,0:T(1,128)}), s32[32,1,2]{2,1,0:T(1,128)S(1)}, u32[]{:S(2)}, u32[]{:S(2)}) %all-to-all-start) | async-done | bytes 288 | tf_op jit(solution)/shard_map/all_to_all | solution.py:291
  17.3 0.5 broadcast.24
  17.9 0.7 reduce.3
  18.5 0.6 reshape.15.asked
  19.2 89.8 %bounces.1 = (bf16[16,75,128]{2,1,0:T(8,128)(2,1)}, bf16[16,75,128]{2,1,0:T(8,128)(2,1)}, f32[2,8,128]{2,1,0:T(8,128)}) custom-call(s32[16,16]{1,0:T(8,128)} %slice_subtract_fusion.near_rows, s32[16,24]{1,0:T(8,128)} %convert_add_fusion.far_rows, s32[64]{0:T(128)} %reshape.15.asked, bf16[16,75,128]{2,1,0:T(8,128)(2,1)} %copy.32.transfer, ...), custom_call_target="tpu_custom_call" | custom-call | tf_op jit(solution)/shard_map/bounces/pallas_call | solution.py:298
  108.9 0.0 copy-start.3
  109.0 0.0 copy-start
  109.0 1.8 %copy.36 = bf16[16,75,128]{2,0,1:T(8,128)(2,1)} copy(bf16[16,75,128]{2,1,0:T(8,128)(2,1)} %get-tuple-element.18) | data formatting | bytes 614400
  110.8 0.0 copy-done.3
  110.8 0.1 reduce_sum.29
  110.9 0.5 broadcast_multiply_fusion
  111.4 0.0 copy-done
  111.4 0.8 copy.37
  (1 shorter events, 0.0 us)
Async XLA Ops:
  0.6 14.0 %copy-start.2 = (f32[16,3,128]{2,0,1:T(8,128)S(1)}, f32[16,3,128]{2,0,1:T(8,128)}, u32[]{:S(2)}) copy-start(f32[16,3,128]{2,0,1:T(8,128)} %param.11) | copy-start | bytes 73732
  0.6 14.7 %copy-start.1 = (bf16[16,75,128]{2,0,1:T(8,128)(2,1)S(1)}, bf16[16,75,128]{2,0,1:T(8,128)(2,1)}, u32[]{:S(2)}) copy-start(bf16[16,75,128]{2,0,1:T(8,128)(2,1)} %param.7) | copy-start | bytes 921604
  2.9 14.5 %all-to-all-start = ((s32[32,1,2]{2,1,0:T(1,128)}), s32[32,1,2]{2,1,0:T(1,128)S(1)}, u32[]{:S(2)}, u32[]{:S(2)}) async-start(s32[32,1,2]{2,1,0:T(1,128)} %copy.31), calls=%async_computation | async-start | bytes 32768 | tf_op jit(solution)/shard_map/all_to_all | solution.py:291
  108.9 1.8 %copy-start.3 = (f32[2,8,128]{2,1,0:T(8,128)S(1)}, f32[2,8,128]{2,1,0:T(8,128)}, u32[]{:S(2)}) copy-start(f32[2,8,128]{2,1,0:T(8,128)} %get-tuple-element.8) | copy-start | bytes 24580
  109.0 2.4 %copy-start = (bf16[16,75,128]{2,1,0:T(8,128)(2,1)S(1)}, bf16[16,75,128]{2,1,0:T(8,128)(2,1)}, u32[]{:S(2)}) copy-start(bf16[16,75,128]{2,1,0:T(8,128)(2,1)} %get-tuple-element.19) | copy-start | bytes 921604
